TPU v7x, 32 devices: a whole 2x2x4 slice. The times are simulated.
32 devices in a mesh: segment: 4 (over z), row: 4 (over y, x), col: 2 (over core).
Axes of the slice: x: 2, y: 2, z: 4, core: 2. Of those that a mesh axis runs over, the one named last changes fastest.
Arguments:
- frames: bfloat16 [2, 64, 32, 128], P(None, 'row', 'col'), may hold values from -6 to 6
- caches: bfloat16 [4, 2, 2, 64, 32, 128], P('segment', None, None, 'row', 'col'), may hold values from -5 to 5
- weights: bfloat16 [4, 2, 3, 3, 3, 128, 128], P('segment'), may hold values from -0.109375 to 0.109375
- biases: float32 [4, 2, 128], P('segment'), may hold values from -0.5 to 0.5
- gains: float32 [4, 2, 128], P('segment'), may hold values from 0.1 to 1.9
Outputs:
- sections: bfloat16 [4, 2, 64, 32, 128], P('segment', None, 'row', 'col')
All inputs are finite; a program needn't handle non-finite values.
Results may differ from a plain program's by a relative error of at most 0.0055.
Values may be sent and summed in bfloat16 or wider, within the bound.
A program may use at most 64 MiB of HBM per device.

v0:
```python
import functools

import jax
import jax.numpy as jnp
from jax import lax
from jax.experimental import pallas as pl
from jax.experimental.pallas import tpu as pltpu
from jax.sharding import PartitionSpec as P

EDGE = 8
STRIP = 2
TAPS = 3
AROUND = [(dr, dc) for dr in (-1, 1, 0) for dc in (-1, 1, 0)]
CENTRE = AROUND.index((0, 0))


def divisor(count, most):
    return max(d for d in range(1, most + 1) if count % d == 0)


def source_range(step, size, width, edge):
    if step == 0:
        return pl.ds(edge, size)
    return pl.ds(edge if step < 0 else edge + size - width, width)


def target_range(step, size, width, edge):
    if step == 0:
        return pl.ds(edge, size)
    return pl.ds(edge + size, width) if step < 0 else pl.ds(edge - width, width)


def norm_act(values, gain_row):
    scale = lax.rsqrt(jnp.mean(values * values, axis=-1, keepdims=True) + 1e-06)
    half = 0.5 * (values * scale * gain_row)
    return half * jnp.tanh(half) + half


def put_taps(store, start, values):
    size, channels = values.shape
    rows = pl.ds(start, size)
    store[rows, 0:channels] = pltpu.roll(values, 1, 0).astype(jnp.bfloat16)
    store[rows, channels : 2 * channels] = values.astype(jnp.bfloat16)
    store[rows, 2 * channels : 3 * channels] = pltpu.roll(values, size - 1, 0).astype(jnp.bfloat16)


def kernel(
    counts,
    frames, caches, weights_in, biases_in, gains_in,
    out,
    weights, biases, gains, x_pad, one_pad, two_pad, taps_one, taps_two,
    held_taps_one, held_taps_two, sum_one, sum_two, inside,
    send_sem, recv_sem, tile_send, tile_recv, local_sem,
):
    segments, tile_rows_n, tile_cols_n = counts
    seg, row, col = (lax.axis_index(name) for name in ("segment", "row", "col"))
    total, rows, cols, channels = frames.shape
    pitch = x_pad.shape[2]

    def exists(dr, dc):
        r, c = row + dr, col + dc
        return (r >= 0) & (r < tile_rows_n) & (c >= 0) & (c < tile_cols_n)

    def device(dz, dr, dc):
        return {"segment": seg + dz, "row": row + dr, "col": col + dc}

    def remote(source, target, halo, send_group, recv_group, dz, which):
        dr, dc = AROUND[which]
        top, left = (0, 0) if dz else (halo, EDGE)
        src_r, src_c = source_range(dr, rows, halo, top), source_range(dc, cols, STRIP, left)
        dst_r, dst_c = target_range(dr, rows, halo, halo), target_range(dc, cols, STRIP, EDGE)
        lead = (slice(None),) * (len(source.shape) - 3)
        return pltpu.make_async_remote_copy(
            src_ref=source.at[lead + (src_r, src_c)],
            dst_ref=target.at[lead + (dst_r, dst_c)],
            send_sem=send_sem.at[send_group, which],
            recv_sem=recv_sem.at[recv_group, which],
            device_id=device(dz, dr, dc),
            device_id_type=pl.DeviceIdType.MESH,
        )

    streams = [
        (one_pad, one_pad, 2, 0, 0, 0),
        (two_pad, two_pad, 1, 1, 1, 0),
    ] + [(x_pad.at[f], x_pad.at[f], 2, 2 + f, 2 + f, 0) for f in range(total)]
    onward = [(out.at[f], x_pad.at[f], 2, 2 + total + f, 2 + f, 1) for f in range(total)]

    step_in = divisor(rows + 4, 5)
    step_one = divisor(rows + 2, 6)
    step_two = divisor(rows, 4)
    chunks = rows // step_two

    def tile_copy(f, chunk):
        start = chunk * step_two
        return pltpu.make_async_remote_copy(
            src_ref=out.at[f, pl.ds(start, step_two)],
            dst_ref=x_pad.at[f, pl.ds(2 + start, step_two), pl.ds(EDGE, cols)],
            send_sem=tile_send.at[f, chunk],
            recv_sem=tile_recv.at[f, chunk],
            device_id=device(1, 0, 0),
            device_id_type=pl.DeviceIdType.MESH,
        )

    def each(stream, allowed, action, steps=(-1, 1, 0)):
        for which, (dr, dc) in enumerate(AROUND):
            if which == CENTRE or dr not in steps:
                continue
            good = exists(dr, dc) if action != "recv" else exists(-dr, -dc)
            if allowed is not None:
                good = good & allowed

            @pl.when(good)
            def _():
                copy = remote(*stream, which)
                if action == "start":
                    copy.start()
                elif action == "send":
                    copy.wait_send()
                else:
                    copy.wait_recv()

    centre_of = lambda pad, halo: pad.at[:, pl.ds(halo, rows), pl.ds(EDGE, cols)]
    first = seg == 0
    later = seg > 0
    more = seg < segments - 1
    own = pltpu.make_async_copy(frames, centre_of(x_pad, 2), local_sem.at[0])
    held_one = pltpu.make_async_copy(caches.at[0], centre_of(one_pad, 2), local_sem.at[1])
    held_two = pltpu.make_async_copy(caches.at[1], centre_of(two_pad, 1), local_sem.at[2])
    parameters = [
        pltpu.make_async_copy(biases_in, biases, local_sem.at[3]),
        pltpu.make_async_copy(gains_in, gains, local_sem.at[4]),
        pltpu.make_async_copy(weights_in.at[0], weights.at[0], local_sem.at[5]),
        pltpu.make_async_copy(weights_in.at[1], weights.at[1], local_sem.at[6]),
    ]

    @pl.when(first)
    def _():
        own.start()

    for copy in [held_one, held_two] + parameters:
        copy.start()

    for pad, halo in ((x_pad, 2), (one_pad, 2), (two_pad, 1)):
        count = pad.shape[0]
        side = pitch - EDGE - cols
        pad[:, 0:halo] = jnp.zeros((count, halo, pitch, channels), pad.dtype)
        pad[:, halo + rows :] = jnp.zeros((count, halo, pitch, channels), pad.dtype)
        pad[:, halo : halo + rows, 0:EDGE] = jnp.zeros((count, rows, EDGE, channels), pad.dtype)
        pad[:, halo : halo + rows, EDGE + cols :] = jnp.zeros((count, rows, side, channels), pad.dtype)

    barrier = pltpu.get_barrier_semaphore()
    arrivals = 0
    for dz in (-1, 0, 1):
        for dr, dc in AROUND:
            if (dz, dr, dc) == (0, 0, 0):
                continue
            good = exists(dr, dc) & (seg + dz >= 0) & (seg + dz < segments)

            @pl.when(good)
            def _():
                pl.semaphore_signal(
                    barrier, inc=1, device_id=device(dz, dr, dc),
                    device_id_type=pl.DeviceIdType.MESH,
                )

            arrivals = arrivals + good.astype(jnp.int32)
    pl.semaphore_wait(barrier, arrivals)

    @pl.when(first)
    def _():
        own.wait()

    for f in range(total):
        each(streams[2 + f], first, "start")
    held_one.wait()
    each(streams[0], None, "start")
    held_two.wait()
    each(streams[1], None, "start")

    cell = lax.broadcasted_iota(jnp.int32, inside.shape, 0)
    cell_row = row * rows + cell // pitch - 1
    cell_col = col * cols + cell % pitch - EDGE
    inside[...] = jnp.where(
        (cell_row >= 0) & (cell_row < rows * tile_rows_n)
        & (cell_col >= 0) & (cell_col < cols * tile_cols_n), 1.0, 0.0,
    )

    def kernel_of(which, *times):
        return jnp.concatenate([weights[which, t] for t in times], axis=1)

    def product(store, start, size, matrix):
        patches = jnp.concatenate(
            [store[pl.ds((start + dh) * pitch, size * pitch), :] for dh in range(TAPS)], axis=1
        )
        return jnp.dot(patches, matrix, preferred_element_type=jnp.float32)

    def load_taps(pad, index, store, size, step, transform):
        for start in range(0, size, step):
            values = pad[index, start : start + step].reshape(step * pitch, channels)
            put_taps(store, start * pitch, transform(values.astype(jnp.float32)))

    def cached(which, pad, store, sums, tap_rows, sum_rows):
        bias = biases[which : which + 1]
        for frame in range(2):
            for low, high in tap_rows:
                step = divisor(high - low, 4)
                for start in range(low, high, step):
                    values = pad[frame, start : start + step].reshape(step * pitch, channels)
                    put_taps(store.at[frame], start * pitch, values.astype(jnp.float32))
        for low, high in sum_rows:
            step = divisor(high - low, 7)
            for start in range(low, high, step):
                part = pl.ds(start * pitch, step * pitch)
                older = product(store.at[0], start, step, kernel_of(which, 0))
                newer = product(store.at[1], start, step, kernel_of(which, 1, 0))
                sums[0, part] = older + newer[:, :channels] + bias
                sums[1, part] = newer[:, channels:] + bias

    for copy in parameters:
        copy.wait()
    held = ((one_pad, held_taps_one, sum_one, 2), (two_pad, held_taps_two, sum_two, 1))
    for which, (pad, store, sums, halo) in enumerate(held):
        end = halo + rows
        each(streams[which], None, "recv", (0,))
        cached(which, pad, store, sums, [(halo, end)], [(halo, end - 2)])
    for which, (pad, store, sums, halo) in enumerate(held):
        end = halo + rows
        each(streams[which], None, "recv", (-1, 1))
        cached(
            which, pad, store, sums,
            [(0, halo), (end, end + halo)], [(0, halo), (end - 2, end + halo - 2)],
        )

    for f in range(total):
        each(streams[2 + f], first, "recv")
        each(onward[f], later, "recv")

        @pl.when(later)
        def _():
            for chunk in range(chunks):
                tile_copy(f, chunk).wait_recv()

        load_taps(x_pad, f, taps_one, rows + 4, step_in, lambda v: norm_act(v, gains[0:1]))
        times = (2, 1) if f == 0 else (2,)
        for start in range(0, rows + 2, step_one):
            part = pl.ds(start * pitch, step_one * pitch)
            fresh = product(taps_one, start, step_one, kernel_of(0, *times))
            hidden = sum_one[f, part] + fresh[:, :channels]
            if f == 0:
                sum_one[1, part] += fresh[:, channels:]
            put_taps(taps_two, start * pitch, norm_act(hidden, gains[1:2]) * inside[part])
        for chunk in [0, chunks - 1] + list(range(1, chunks - 1)) if chunks > 1 else [0]:
            start = chunk * step_two
            part = pl.ds(start * pitch, step_two * pitch)
            fresh = product(taps_two, start, step_two, kernel_of(1, *times))
            branch = sum_two[f, part] + fresh[:, :channels]
            if f == 0:
                sum_two[1, part] += fresh[:, channels:]
            branch = branch.reshape(step_two, pitch, channels)[:, EDGE : EDGE + cols]
            inputs = x_pad[f, 2 + start : 2 + start + step_two, EDGE : EDGE + cols]
            out[f, start : start + step_two] = (inputs.astype(jnp.float32) + branch).astype(out.dtype)
            if chunk == 0:
                each(onward[f], more, "start", (-1,))
            if chunk == chunks - 1:
                each(onward[f], more, "start", (1,))

            @pl.when(more)
            def _():
                tile_copy(f, chunk).start()

        each(onward[f], more, "start", (0,))

    for stream in streams[:2]:
        each(stream, None, "send")
    for f in range(total):
        each(streams[2 + f], first, "send")
        each(onward[f], more, "send")

        @pl.when(more)
        def _():
            for chunk in range(chunks):
                tile_copy(f, chunk).wait_send()


def solution(mesh):
    counts = tuple(mesh.shape[name] for name in ("segment", "row", "col"))

    def on_device(frames, caches, weights, biases, gains):
        total, rows, cols, channels = frames.shape
        pitch = -(-(cols + 2 * EDGE) // 16) * 16
        bf16, f32 = jnp.bfloat16, jnp.float32
        vmem = pl.BlockSpec(memory_space=pltpu.VMEM)
        taps = weights.reshape(2, TAPS, TAPS * TAPS * channels, channels)
        result = pl.pallas_call(
            functools.partial(kernel, counts),
            out_shape=pltpu.VMEM(frames.shape, bf16),
            in_specs=[pl.BlockSpec(memory_space=pl.ANY)] * 5,
            out_specs=vmem,
            scratch_shapes=[
                pltpu.VMEM(taps.shape, bf16),
                pltpu.VMEM(biases.shape[1:], f32),
                pltpu.VMEM(gains.shape[1:], f32),
                pltpu.VMEM((total, rows + 4, pitch, channels), bf16),
                pltpu.VMEM((2, rows + 4, pitch, channels), bf16),
                pltpu.VMEM((2, rows + 2, pitch, channels), bf16),
                pltpu.VMEM(((rows + 4) * pitch, TAPS * channels), bf16),
                pltpu.VMEM(((rows + 2) * pitch, TAPS * channels), bf16),
                pltpu.VMEM((2, (rows + 4) * pitch, TAPS * channels), bf16),
                pltpu.VMEM((2, (rows + 2) * pitch, TAPS * channels), bf16),
                pltpu.VMEM((total, (rows + 2) * pitch, channels), f32),
                pltpu.VMEM((total, rows * pitch, channels), f32),
                pltpu.VMEM(((rows + 2) * pitch, channels), f32),
                pltpu.SemaphoreType.DMA((2 + 2 * total, 9)),
                pltpu.SemaphoreType.DMA((2 + total, 9)),
                pltpu.SemaphoreType.DMA((total, divisor(rows, 16))),
                pltpu.SemaphoreType.DMA((total, divisor(rows, 16))),
                pltpu.SemaphoreType.DMA((7,)),
            ],
            compiler_params=pltpu.CompilerParams(collective_id=0, has_side_effects=True),
        )(frames, caches[0], taps, biases[0], gains[0])
        return result[None]

    in_specs = (
        P(None, "row", "col", None),
        P("segment", None, None, "row", "col", None),
        P("segment", None, None, None, None, None, None),
        P("segment", None, None),
        P("segment", None, None),
    )
    out_specs = P("segment", None, "row", "col", None)
    return jax.shard_map(
        on_device, mesh=mesh, in_specs=in_specs, out_specs=out_specs, check_vma=False
    )
```

profile of v0, /device:TPU:29, one launch (start us, length us, event | category | flops | bytes accessed | tf_op | source)
XLA Modules:
  0.0 27.3 jit_solution(3995826039751870974)
XLA Ops:
  0.0 26.7 %shard_map.55 = bf16[2,16,16,128]{3,2,1,0:T(8,128)(2,1)S(1)} custom-call(bf16[2,16,16,128]{3,2,1,0:T(8,128)(2,1)} %frames.1, bf16[2,2,16,16,128]{4,3,2,1,0:T(8,128)(2,1)} %bitcast.7, bf16[2,3,1152,128]{3,2,1,0:T(8,128)(2,1)} %bitcast.6, f32[2,128]{1,0:T(2,128)} %bitcast.8, f32[2,128]{1,0:T(2,128)} %bitcast.9), custom_call_target="tpu_custom_call" | custom-call | tf_op jit(solution)/shard_map/pallas_call | solution.py:294
  26.7 0.7 %copy.7 = bf16[1,2,16,16,128]{4,3,2,1,0:T(8,128)(2,1)} copy(bf16[1,2,16,16,128]{4,3,2,1,0:T(8,128)(2,1)S(1)} %bitcast.5) | data formatting | bytes 262144
where the time goes:
time: 27.5 us; the launch traced here: 27.3 us
  Pallas kernels  26.7 us (97%)
  local copies, waits for them, and re-layouts  0.66 us (2%)
    pallas_call x1, Pallas kernels, on_device(): pl.pallas_call(functools.partial(kernel, counts), out_shape=pltpu.VMEM(fr...  26.7 us
    unnamed x1, local copies, waits for them, and re-layouts  0.66 us

commit v1 on v0

v1 whole, which is shorter than its diff:
```python
import functools

import jax
import jax.numpy as jnp
from jax import lax
from jax.experimental import pallas as pl
from jax.experimental.pallas import tpu as pltpu
from jax.sharding import PartitionSpec as P

EDGE = 8
STRIP = 2
TAPS = 3
AROUND = [(dr, dc) for dr in (-1, 1, 0) for dc in (0, -1, 1) if (dr, dc) != (0, 0)]
MID, OUTER = 0, 1


def neighbours(count):
    return {1: (0,), 2: (1,)}.get(count, (1, 2))


def norm_act(values, gain_row):
    scale = lax.rsqrt(jnp.mean(values * values, axis=-1, keepdims=True) + 1e-06)
    half = 0.5 * (values * scale * gain_row)
    return half * jnp.tanh(half) + half


def shifted(values):
    size = values.shape[0]
    return pltpu.roll(values, 1, 0), values, pltpu.roll(values, size - 1, 0)


def kernel(
    counts,
    frames, caches, weights_in, biases_in, gains_in,
    out,
    weights, biases, gains, x_pad, one_pad, two_pad, taps_one, taps_two,
    held_taps_one, held_taps_two, sum_one, sum_two, inside,
    send_sem, recv_sem, local_sem, ready_sem,
):
    segments, tile_rows_n, tile_cols_n = counts
    seg, row, col = (lax.axis_index(name) for name in ("segment", "row", "col"))
    total, rows, cols, channels = frames.shape
    pitch = cols + EDGE
    first = seg == 0
    later = seg > 0
    more = seg < segments - 1

    def exists(dr, dc):
        r, c = row + dr, col + dc
        return (r >= 0) & (r < tile_rows_n) & (c >= 0) & (c < tile_cols_n)

    def device(dz, dr, dc):
        return {"segment": seg + dz, "row": row + dr, "col": col + dc}

    def number(flag):
        return flag.astype(jnp.int32)

    ups = number(row > 0) + number(row < tile_rows_n - 1)
    sides = number(col > 0) + number(col < tile_cols_n - 1)

    def local(source, target, which):
        return pltpu.make_async_copy(source, target, local_sem.at[which])

    def source_rows(dr, base, halo):
        if dr == 0:
            return pl.ds(base, rows)
        return pl.ds(base if dr < 0 else base + rows - halo, halo)

    def source_cols(dc, base):
        if dc == 0:
            return pl.ds(base, cols)
        return pl.ds(base if dc < 0 else base + cols - STRIP, STRIP)

    def target_rows(dr, dc, halo):
        skip = 1 if dc < 0 else 0
        if dr == 0:
            return pl.ds(halo + skip, rows)
        return pl.ds((halo + rows if dr < 0 else 0) + skip, halo)

    def target_cols(dc):
        if dc == 0:
            return pl.ds(EDGE, cols)
        return pl.ds(0, STRIP) if dc < 0 else pl.ds(EDGE - STRIP, STRIP)

    def remote(source, target, halo, send, recv, dz, dr, dc):
        top, left = (0, 0) if dz else (halo, EDGE)
        lead = (slice(None),) * (len(source.shape) - 3)
        group = OUTER if dr else MID
        return pltpu.make_async_remote_copy(
            src_ref=source.at[lead + (source_rows(dr, top, halo), source_cols(dc, left))],
            dst_ref=target.at[lead + (target_rows(dr, dc, halo), target_cols(dc))],
            send_sem=send_sem.at[send, group],
            recv_sem=recv_sem.at[recv, group],
            device_id=device(dz, dr, dc),
            device_id_type=pl.DeviceIdType.MESH,
        )

    held = [(one_pad, one_pad, 2, 0, 0, 0), (two_pad, two_pad, 1, 1, 1, 0)]
    begin = [(x_pad.at[f], x_pad.at[f], 2, 2 + f, 2 + f, 0) for f in range(total)]
    onward = [(out.at[f], x_pad.at[f], 2, 2 + total + f, 2 + f, 1) for f in range(total)]

    def start(stream, allowed, outer):
        for dr, dc in AROUND:
            if dr not in outer:
                continue
            good = exists(dr, dc)
            if allowed is not None:
                good = good & allowed

            @pl.when(good)
            def _():
                remote(*stream, dr, dc).start()

    def settle(sem, view, options, allowed):
        for up in options[0]:
            for side in options[1]:
                shape = view(up, side)
                if shape is None:
                    continue
                good = (ups == up) & (sides == side)
                if allowed is not None:
                    good = good & allowed

                @pl.when(good)
                def _():
                    pltpu.make_async_copy(shape, shape, sem).wait()

    up_options, side_options = neighbours(tile_rows_n), neighbours(tile_cols_n)

    def cut(ref, height, width):
        if height == 0 or width == 0:
            return None
        lead = (slice(None),) * (len(ref.shape) - 3)
        return ref.at[lead + (pl.ds(0, height), pl.ds(0, width))]

    def settle_group(sems, which, stream, group, allowed, centre):
        ref, halo = stream[1], stream[2]
        middle = cols if centre else 0
        if group == MID:
            view = lambda up, side: cut(ref, rows, middle + STRIP * side)
        else:
            view = lambda up, side: cut(ref, halo * up, cols + STRIP * side)
        settle(sems.at[which, group], view, (up_options, side_options), allowed)

    def received(stream, group, allowed=None, centre=False):
        settle_group(recv_sem, stream[4], stream, group, allowed, centre)

    def sent(stream, allowed=None, centre=False):
        for group in (MID, OUTER):
            settle_group(send_sem, stream[3], stream, group, allowed, centre)

    edge = rows // 4 if rows % 4 == 0 else rows // 2
    pieces = [(0, edge), (rows - edge, edge)] + ([(edge, rows - 2 * edge)] if rows > 2 * edge else [])

    def tile_copy(f, low, size):
        return pltpu.make_async_remote_copy(
            src_ref=out.at[f, pl.ds(low, size)],
            dst_ref=x_pad.at[f, pl.ds(2 + low, size), pl.ds(EDGE, cols)],
            send_sem=send_sem.at[2 + total + f, MID],
            recv_sem=recv_sem.at[2 + f, MID],
            device_id=device(1, 0, 0),
            device_id_type=pl.DeviceIdType.MESH,
        )

    centre_of = lambda pad, halo: pad.at[:, pl.ds(halo, rows), pl.ds(EDGE, cols)]
    own = local(frames, centre_of(x_pad, 2), 0)
    held_copies = [local(caches.at[0], centre_of(one_pad, 2), 1), local(caches.at[1], centre_of(two_pad, 1), 2)]
    parameters = [
        local(biases_in, biases, 3),
        local(gains_in, gains, 4),
        local(weights_in.at[0], weights.at[0], 5),
        local(weights_in.at[1], weights.at[1], 6),
    ]

    @pl.when(first)
    def _():
        own.start()

    for copy in held_copies + parameters:
        copy.start()

    for pad, halo in ((x_pad, 2), (one_pad, 2), (two_pad, 1)):
        count, height = pad.shape[0], pad.shape[1]
        pad[:, :, 0:EDGE] = jnp.zeros((count, height, EDGE, channels), pad.dtype)
        pad[:, 0:halo, EDGE:] = jnp.zeros((count, halo, cols, channels), pad.dtype)
        pad[:, halo + rows :, EDGE:] = jnp.zeros((count, height - halo - rows, cols, channels), pad.dtype)

    def signal_all(semaphore, steps):
        for dz in steps:
            for dr, dc in AROUND + [(0, 0)]:
                if (dz, dr, dc) == (0, 0, 0):
                    continue

                @pl.when(exists(dr, dc) & (seg + dz >= 0) & (seg + dz < segments))
                def _():
                    pl.semaphore_signal(
                        semaphore, inc=1, device_id=device(dz, dr, dc),
                        device_id_type=pl.DeviceIdType.MESH,
                    )

    plane = (ups + 1) * (sides + 1)
    barrier = pltpu.get_barrier_semaphore()
    signal_all(barrier, (0, 1))
    pl.semaphore_wait(barrier, plane - 1 + plane * number(later))

    @pl.when(first)
    def _():
        own.wait()

    start(begin[0], first, (-1, 1, 0))
    held_copies[0].wait()
    start(held[0], None, (-1, 1, 0))
    held_copies[1].wait()
    start(held[1], None, (-1, 1, 0))
    for f in range(1, total):
        start(begin[f], first, (-1, 1, 0))
    signal_all(ready_sem, (-1,))

    cell = lax.broadcasted_iota(jnp.int32, inside.shape, 0)
    place = cell % pitch
    wrapped = place < EDGE // 2
    cell_row = row * rows + cell // pitch - 1 - number(wrapped)
    cell_col = col * cols + place - EDGE + jnp.where(wrapped, EDGE + cols, 0)
    inside[...] = jnp.where(
        (cell_row >= 0) & (cell_row < rows * tile_rows_n)
        & (cell_col >= 0) & (cell_col < cols * tile_cols_n), 1.0, 0.0,
    )

    def kernel_of(which, *times):
        return jnp.concatenate([weights[which, t] for t in times], axis=1)

    def patches(store, step, parts):
        return jnp.concatenate(
            [
                jnp.concatenate([store[pl.ds(low + dh * step, size), :] for low, size in parts], axis=0)
                for dh in range(TAPS)
            ],
            axis=1,
        )

    def product(store, step, parts, matrix):
        return jnp.dot(patches(store, step, parts), matrix, preferred_element_type=jnp.float32)

    def flat(pad, index, low, high):
        values = pad[index, low:high].astype(jnp.float32)
        return values.reshape((high - low) * pitch, channels)

    def put_all(store, low, values, skip, size):
        for tap, part in enumerate(shifted(values)):
            store[pl.ds(low, size), tap * channels : (tap + 1) * channels] = (
                part[skip : skip + size].astype(jnp.bfloat16)
            )

    def put_tile(store, low, values, height):
        for tap, part in enumerate(shifted(values)):
            part = part[: height * pitch].reshape(height, pitch, channels)[:, EDGE:]
            store[pl.ds(low * cols, height * cols), tap * channels : (tap + 1) * channels] = (
                part.reshape(height * cols, channels).astype(jnp.bfloat16)
            )

    def add_cached(which, store, sums, step, parts):
        bias = biases[which : which + 1]
        older = product(store.at[0], step, parts, kernel_of(which, 0))
        newer = product(store.at[1], step, parts, kernel_of(which, 1, 0))
        at = 0
        for low, size in parts:
            here = slice(at, at + size)
            sums[0, pl.ds(low, size)] = older[here] + newer[here, :channels] + bias
            sums[1, pl.ds(low, size)] = newer[here, channels:] + bias
            at += size

    for copy in parameters:
        copy.wait()

    whole = sum_one.shape[1]
    brim = -(-(3 * pitch + EDGE) // 16) * 16
    rest = (rows - 1) * pitch // 16 * 16
    received(held[0], MID)
    for frame in range(2):
        put_all(
            held_taps_one.at[frame], 3 * pitch, flat(one_pad, frame, 3, rows + 2), 0, (rows - 1) * pitch
        )
    low = 3 * pitch
    add_cached(0, held_taps_one, sum_one, pitch, [(low, (rows - 1) * pitch + EDGE - low)])
    received(held[1], MID)
    for frame in range(2):
        put_tile(held_taps_two.at[frame], 2, flat(two_pad, frame, 2, rows + 1), rows - 2)
    add_cached(1, held_taps_two, sum_two, cols, [(2 * cols, (rows - 4) * cols)])

    received(held[0], OUTER)
    for frame in range(2):
        put_all(held_taps_one.at[frame], 0, flat(one_pad, frame, 0, 5), 0, brim)
        values = flat(one_pad, frame, rows, rows + 5)
        put_all(held_taps_one.at[frame], rows * pitch + EDGE, values, EDGE, 5 * pitch - EDGE)
    add_cached(0, held_taps_one, sum_one, pitch, [(0, brim), (rest, whole - rest)])
    received(held[1], OUTER)
    for frame in range(2):
        put_tile(held_taps_two.at[frame], 0, flat(two_pad, frame, 0, 3), 2)
        put_tile(held_taps_two.at[frame], rows, flat(two_pad, frame, rows, rows + 3), 2)
    add_cached(1, held_taps_two, sum_two, cols, [(0, 2 * cols), ((rows - 2) * cols, 2 * cols)])

    @pl.when(more)
    def _():
        pl.semaphore_wait(ready_sem, plane)

    half = (rows + 2) // 4 * 2
    blocks = [(0, half), (half, rows + 2 - half)]

    for f in range(total):
        for group in (MID, OUTER):
            received(begin[f], group, first)
            received(onward[f], group, later, group == MID)

        values = norm_act(flat(x_pad, f, 0, rows + 5), gains[0:1])
        put_all(taps_one, 0, values, 0, (rows + 5) * pitch)
        times = (2, 1) if f == 0 else (2,)
        for low, height in blocks:
            last = low + height == rows + 2
            size = whole - low * pitch if last else height * pitch + EDGE
            part = pl.ds(low * pitch, size)
            fresh = product(taps_one, pitch, [(low * pitch, size)], kernel_of(0, *times))
            hidden = sum_one[f, part] + fresh[:, :channels]
            if f == 0:
                keep = size if last else height * pitch
                sum_one[1, pl.ds(low * pitch, keep)] += fresh[:keep, channels:]
            put_tile(taps_two, low, norm_act(hidden, gains[1:2]) * inside[part], height)
        for group in (pieces[:2], pieces[2:]):
            if not group:
                continue
            parts = [(low * cols, size * cols) for low, size in group]
            fresh = product(taps_two, cols, parts, kernel_of(1, *times))
            at = 0
            for low, size in group:
                here = slice(at, at + size * cols)
                part = pl.ds(low * cols, size * cols)
                branch = sum_two[f, part] + fresh[here, :channels]
                if f == 0:
                    sum_two[1, part] += fresh[here, channels:]
                inputs = x_pad[f, 2 + low : 2 + low + size, EDGE:].astype(jnp.float32)
                out[f, low : low + size] = (inputs + branch.reshape(size, cols, channels)).astype(out.dtype)
                at += size * cols
            if group[0][0] == 0:
                start(onward[f], more, (-1, 1))
            if group[-1] is pieces[-1]:
                start(onward[f], more, (0,))

            @pl.when(more)
            def _():
                for low, size in group:
                    tile_copy(f, low, size).start()

    for stream in held:
        sent(stream)
    for f in range(total):
        sent(begin[f], first)
        sent(onward[f], more, True)


def solution(mesh):
    counts = tuple(mesh.shape[name] for name in ("segment", "row", "col"))

    def on_device(frames, caches, weights, biases, gains):
        total, rows, cols, channels = frames.shape
        pitch = cols + EDGE
        whole = -(-((rows + 2) * pitch + EDGE) // 16) * 16
        bf16, f32 = jnp.bfloat16, jnp.float32
        vmem = pl.BlockSpec(memory_space=pltpu.VMEM)
        taps = weights.reshape(2, TAPS, TAPS * TAPS * channels, channels)
        result = pl.pallas_call(
            functools.partial(kernel, counts),
            out_shape=pltpu.VMEM(frames.shape, bf16),
            in_specs=[pl.BlockSpec(memory_space=pl.ANY)] * 5,
            out_specs=vmem,
            scratch_shapes=[
                pltpu.VMEM(taps.shape, bf16),
                pltpu.VMEM(biases.shape[1:], f32),
                pltpu.VMEM(gains.shape[1:], f32),
                pltpu.VMEM((total, rows + 5, pitch, channels), bf16),
                pltpu.VMEM((2, rows + 5, pitch, channels), bf16),
                pltpu.VMEM((2, rows + 3, pitch, channels), bf16),
                pltpu.VMEM(((rows + 5) * pitch, TAPS * channels), bf16),
                pltpu.VMEM(((rows + 2) * cols, TAPS * channels), bf16),
                pltpu.VMEM((2, (rows + 5) * pitch, TAPS * channels), bf16),
                pltpu.VMEM((2, (rows + 2) * cols, TAPS * channels), bf16),
                pltpu.VMEM((total, whole, channels), f32),
                pltpu.VMEM((total, rows * cols, channels), f32),
                pltpu.VMEM((whole, channels), f32),
                pltpu.SemaphoreType.DMA((2 + 2 * total, 2)),
                pltpu.SemaphoreType.DMA((2 + total, 2)),
                pltpu.SemaphoreType.DMA((7,)),
                pltpu.SemaphoreType.REGULAR,
            ],
            compiler_params=pltpu.CompilerParams(collective_id=0, has_side_effects=True),
        )(frames, caches[0], taps, biases[0], gains[0])
        return result[None]

    in_specs = (
        P(None, "row", "col", None),
        P("segment", None, None, "row", "col", None),
        P("segment", None, None, None, None, None, None),
        P("segment", None, None),
        P("segment", None, None),
    )
    out_specs = P("segment", None, "row", "col", None)
    return jax.shard_map(
        on_device, mesh=mesh, in_specs=in_specs, out_specs=out_specs, check_vma=False
    )
```

time: 27.5 us -> 24.4 us (0.89); the launches traced: 27.3 us -> 23.9 us
  Pallas kernels: 26.7 us -> 23.3 us
    pallas_call x1, Pallas kernels: 26.7 us -> 23.3 us  [on_device(): pl.pallas_call(functools.partial(kernel, counts), out_shape=pltpu.VMEM(fr...]
where the time goes in v1:
time: 24.4 us; the launch traced here: 23.9 us
  Pallas kernels  23.3 us (95%)
  local copies, waits for them, and re-layouts  0.66 us (3%)
    pallas_call x1, Pallas kernels, on_device(): pl.pallas_call(functools.partial(kernel, counts), out_shape=pltpu.VMEM(fr...  23.3 us
    unnamed x1, local copies, waits for them, and re-layouts  0.66 us

profile of v1, /device:TPU:29, one launch (start us, length us, event | category | flops | bytes accessed | tf_op | source)
XLA Modules:
  0.0 23.9 jit_solution(1745649065530928904)
XLA Ops:
  0.0 23.3 %shard_map.55 = bf16[2,16,16,128]{3,2,1,0:T(8,128)(2,1)S(1)} custom-call(bf16[2,16,16,128]{3,2,1,0:T(8,128)(2,1)} %frames.1, bf16[2,2,16,16,128]{4,3,2,1,0:T(8,128)(2,1)} %bitcast.7, bf16[2,3,1152,128]{3,2,1,0:T(8,128)(2,1)} %bitcast.6, f32[2,128]{1,0:T(2,128)} %bitcast.8, f32[2,128]{1,0:T(2,128)} %bitcast.9), custom_call_target="tpu_custom_call" | custom-call | tf_op jit(solution)/shard_map/pallas_call | solution.py:369
  23.3 0.7 %copy.7 = bf16[1,2,16,16,128]{4,3,2,1,0:T(8,128)(2,1)} copy(bf16[1,2,16,16,128]{4,3,2,1,0:T(8,128)(2,1)S(1)} %bitcast.5) | data formatting | bytes 262144

commit v2 on v1

--- a/solution.py
+++ b/solution.py
@@ -149,8 +149,7 @@
         for group in (MID, OUTER):
             settle_group(send_sem, stream[3], stream, group, allowed, centre)
 
-    edge = rows // 4 if rows % 4 == 0 else rows // 2
-    pieces = [(0, edge), (rows - edge, edge)] + ([(edge, rows - 2 * edge)] if rows > 2 * edge else [])
+    edge = rows // 4
 
     def tile_copy(f, low, size):
         return pltpu.make_async_remote_copy(
@@ -274,7 +273,7 @@
 
     whole = sum_one.shape[1]
     brim = -(-(3 * pitch + EDGE) // 16) * 16
-    rest = (rows - 1) * pitch // 16 * 16
+    rest = (rows - 1) * pitch
     received(held[0], MID)
     for frame in range(2):
         put_all(
@@ -287,73 +286,122 @@
         put_tile(held_taps_two.at[frame], 2, flat(two_pad, frame, 2, rows + 1), rows - 2)
     add_cached(1, held_taps_two, sum_two, cols, [(2 * cols, (rows - 4) * cols)])
 
-    received(held[0], OUTER)
-    for frame in range(2):
-        put_all(held_taps_one.at[frame], 0, flat(one_pad, frame, 0, 5), 0, brim)
-        values = flat(one_pad, frame, rows, rows + 5)
-        put_all(held_taps_one.at[frame], rows * pitch + EDGE, values, EDGE, 5 * pitch - EDGE)
-    add_cached(0, held_taps_one, sum_one, pitch, [(0, brim), (rest, whole - rest)])
-    received(held[1], OUTER)
-    for frame in range(2):
-        put_tile(held_taps_two.at[frame], 0, flat(two_pad, frame, 0, 3), 2)
-        put_tile(held_taps_two.at[frame], rows, flat(two_pad, frame, rows, rows + 3), 2)
-    add_cached(1, held_taps_two, sum_two, cols, [(0, 2 * cols), ((rows - 2) * cols, 2 * cols)])
-
-    @pl.when(more)
+    @pl.when(more & later)
     def _():
         pl.semaphore_wait(ready_sem, plane)
 
-    half = (rows + 2) // 4 * 2
-    blocks = [(0, half), (half, rows + 2 - half)]
-
-    for f in range(total):
+    def held_edges():
+        for frame in range(2):
+            put_all(held_taps_one.at[frame], 0, flat(one_pad, frame, 0, 5), 0, brim)
+            values = flat(one_pad, frame, rows, rows + 5)
+            put_all(held_taps_one.at[frame], rows * pitch + EDGE, values, EDGE, 5 * pitch - EDGE)
+        add_cached(0, held_taps_one, sum_one, pitch, [(0, brim), (rest, whole - rest)])
+        for frame in range(2):
+            put_tile(held_taps_two.at[frame], 0, flat(two_pad, frame, 0, 3), 2)
+            put_tile(held_taps_two.at[frame], rows, flat(two_pad, frame, rows, rows + 3), 2)
+        add_cached(1, held_taps_two, sum_two, cols, [(0, 2 * cols), ((rows - 2) * cols, 2 * cols)])
+
+    def matrix(which, f):
+        return kernel_of(which, *((2, 1) if f == 0 else (2,)))
+
+    def act(f, low, high):
+        return norm_act(flat(x_pad, f, low, high), gains[0:1])
+
+    def conv_one(f, groups, again=False):
+        parts = [
+            (low * pitch, whole - low * pitch if low + height == rows + 2 else height * pitch + EDGE)
+            for low, height in groups
+        ]
+        fresh = product(taps_one, pitch, parts, matrix(0, f))
+        at = 0
+        for (low, height), (base, size) in zip(groups, parts):
+            part = pl.ds(base, size)
+            hidden = sum_one[f, part] + fresh[at : at + size, :channels]
+            if f == 0:
+                keep = size if low + height == rows + 2 or again else height * pitch
+                sum_one[1, pl.ds(base, keep)] += fresh[at : at + keep, channels:]
+            put_tile(taps_two, low, norm_act(hidden, gains[1:2]) * inside[part], height)
+            at += size
+
+    def conv_two(f, groups):
+        parts = [(low * cols, size * cols) for low, size in groups]
+        fresh = product(taps_two, cols, parts, matrix(1, f))
+        at = 0
+        for low, size in groups:
+            here = slice(at, at + size * cols)
+            part = pl.ds(low * cols, size * cols)
+            branch = sum_two[f, part] + fresh[here, :channels]
+            if f == 0:
+                sum_two[1, part] += fresh[here, channels:]
+            inputs = x_pad[f, 2 + low : 2 + low + size, EDGE:].astype(jnp.float32)
+            out[f, low : low + size] = (inputs + branch.reshape(size, cols, channels)).astype(out.dtype)
+            at += size * cols
+
+    def send_tile(f, groups):
+        @pl.when(more)
+        def _():
+            for low, size in groups:
+                tile_copy(f, low, size).start()
+
+    borders = [(0, edge), (rows - edge, edge)]
+    middle = [(edge, rows - 2 * edge)]
+
+    @pl.when(first)
+    def _():
+        received(begin[0], MID)
+        put_all(taps_one, 3 * pitch, act(0, 3, rows + 2), 0, (rows - 1) * pitch)
+        conv_one(0, [(3, rows - 4)])
+        conv_two(0, middle)
+        if segments > 1:
+            pl.semaphore_wait(ready_sem, plane)
+        send_tile(0, middle)
+        for stream in held + begin[:1]:
+            received(stream, OUTER)
+        held_edges()
+        put_all(taps_one, 0, act(0, 0, 5), 0, brim)
+        put_all(taps_one, rows * pitch + EDGE, act(0, rows, rows + 5), EDGE, 5 * pitch - EDGE)
+        conv_one(0, [(0, 3), (rows - 1, 3)], again=True)
+        conv_two(0, borders)
+
+    @pl.when(later)
+    def _():
+        for stream in held:
+            received(stream, OUTER)
+        held_edges()
+        received(onward[0], OUTER)
+        received(onward[0], MID, None, True)
+        put_all(taps_one, 0, act(0, 0, rows + 5), 0, (rows + 5) * pitch)
+        conv_one(0, [(0, edge + 2), (rows - edge, edge + 2)])
+        conv_two(0, borders)
+
+    start(onward[0], more, (-1, 1))
+    send_tile(0, borders)
+
+    @pl.when(later)
+    def _():
+        conv_one(0, [(edge + 2, rows - 2 * edge - 2)])
+        conv_two(0, middle)
+        send_tile(0, middle)
+
+    start(onward[0], more, (0,))
+
+    for f in range(1, total):
         for group in (MID, OUTER):
             received(begin[f], group, first)
             received(onward[f], group, later, group == MID)
-
-        values = norm_act(flat(x_pad, f, 0, rows + 5), gains[0:1])
-        put_all(taps_one, 0, values, 0, (rows + 5) * pitch)
-        times = (2, 1) if f == 0 else (2,)
-        for low, height in blocks:
-            last = low + height == rows + 2
-            size = whole - low * pitch if last else height * pitch + EDGE
-            part = pl.ds(low * pitch, size)
-            fresh = product(taps_one, pitch, [(low * pitch, size)], kernel_of(0, *times))
-            hidden = sum_one[f, part] + fresh[:, :channels]
-            if f == 0:
-                keep = size if last else height * pitch
-                sum_one[1, pl.ds(low * pitch, keep)] += fresh[:keep, channels:]
-            put_tile(taps_two, low, norm_act(hidden, gains[1:2]) * inside[part], height)
-        for group in (pieces[:2], pieces[2:]):
-            if not group:
-                continue
-            parts = [(low * cols, size * cols) for low, size in group]
-            fresh = product(taps_two, cols, parts, kernel_of(1, *times))
-            at = 0
-            for low, size in group:
-                here = slice(at, at + size * cols)
-                part = pl.ds(low * cols, size * cols)
-                branch = sum_two[f, part] + fresh[here, :channels]
-                if f == 0:
-                    sum_two[1, part] += fresh[here, channels:]
-                inputs = x_pad[f, 2 + low : 2 + low + size, EDGE:].astype(jnp.float32)
-                out[f, low : low + size] = (inputs + branch.reshape(size, cols, channels)).astype(out.dtype)
-                at += size * cols
-            if group[0][0] == 0:
-                start(onward[f], more, (-1, 1))
-            if group[-1] is pieces[-1]:
-                start(onward[f], more, (0,))
-
-            @pl.when(more)
-            def _():
-                for low, size in group:
-                    tile_copy(f, low, size).start()
+        put_all(taps_one, 0, act(f, 0, rows + 5), 0, (rows + 5) * pitch)
+        conv_one(f, [(0, rows + 2)])
+        conv_two(f, [(0, rows)])
+        sent(onward[f - 1], more, True)
+        start(onward[f], more, (-1, 1))
+        send_tile(f, borders + middle)
+        start(onward[f], more, (0,))
 
     for stream in held:
         sent(stream)
     for f in range(total):
         sent(begin[f], first)
-        sent(onward[f], more, True)
+    sent(onward[total - 1], more, True)
 
 
 def solution(mesh):

time: 24.4 us -> 23.5 us (0.963); the launches traced: 23.9 us -> 23.4 us
  Pallas kernels: 23.3 us -> 22.7 us
    pallas_call x1, Pallas kernels: 23.3 us -> 22.7 us  [on_device(): pl.pallas_call(functools.partial(kernel, counts), out_shape=pltpu.VMEM(fr...]
where the time goes in v2:
time: 23.5 us; the launch traced here: 23.4 us
  Pallas kernels  22.7 us (97%)
  local copies, waits for them, and re-layouts  0.66 us (3%)
    pallas_call x1, Pallas kernels, on_device(): pl.pallas_call(functools.partial(kernel, counts), out_shape=pltpu.VMEM(fr...  22.7 us
    unnamed x1, local copies, waits for them, and re-layouts  0.66 us

profile of v2, /device:TPU:29, one launch (start us, length us, event | category | flops | bytes accessed | tf_op | source)
XLA Modules:
  0.0 23.4 jit_solution(16807622050226091771)
XLA Ops:
  0.0 22.7 %shard_map.55 = bf16[2,16,16,128]{3,2,1,0:T(8,128)(2,1)S(1)} custom-call(bf16[2,16,16,128]{3,2,1,0:T(8,128)(2,1)} %frames.1, bf16[2,2,16,16,128]{4,3,2,1,0:T(8,128)(2,1)} %bitcast.7, bf16[2,3,1152,128]{3,2,1,0:T(8,128)(2,1)} %bitcast.6, f32[2,128]{1,0:T(2,128)} %bitcast.8, f32[2,128]{1,0:T(2,128)} %bitcast.9), custom_call_target="tpu_custom_call" | custom-call | tf_op jit(solution)/shard_map/pallas_call | solution.py:417
  22.7 0.7 %copy.7 = bf16[1,2,16,16,128]{4,3,2,1,0:T(8,128)(2,1)} copy(bf16[1,2,16,16,128]{4,3,2,1,0:T(8,128)(2,1)S(1)} %bitcast.5) | data formatting | bytes 262144

commit v3 on v2

--- a/solution.py
+++ b/solution.py
@@ -104,7 +104,7 @@
             if dr not in outer:
                 continue
             good = exists(dr, dc)
-            if allowed is not None:
+            if allowed is not True:
                 good = good & allowed
 
             @pl.when(good)
@@ -145,8 +145,8 @@
     def received(stream, group, allowed=None, centre=False):
         settle_group(recv_sem, stream[4], stream, group, allowed, centre)
 
-    def sent(stream, allowed=None, centre=False):
-        for group in (MID, OUTER):
+    def sent(stream, allowed=None, centre=False, groups=(MID, OUTER)):
+        for group in groups:
             settle_group(send_sem, stream[3], stream, group, allowed, centre)
 
     edge = rows // 4
@@ -206,11 +206,18 @@
     def _():
         own.wait()
 
-    start(begin[0], first, (-1, 1, 0))
-    held_copies[0].wait()
-    start(held[0], None, (-1, 1, 0))
-    held_copies[1].wait()
-    start(held[1], None, (-1, 1, 0))
+    for copy in held_copies:
+        copy.wait()
+    early = [(begin[0], first), (held[0], True), (held[1], True)]
+    even = row % 2 == 0
+    for stream, allowed in early:
+        start(stream, even & allowed, (-1,))
+        start(stream, ~even & allowed, (1,))
+    for stream, allowed in early:
+        start(stream, allowed, (0,))
+    for stream, allowed in early:
+        start(stream, even & allowed, (1,))
+        start(stream, ~even & allowed, (-1,))
     for f in range(1, total):
         start(begin[f], first, (-1, 1, 0))
     signal_all(ready_sem, (-1,))
@@ -290,12 +297,14 @@
     def _():
         pl.semaphore_wait(ready_sem, plane)
 
-    def held_edges():
+    def held_edge_one():
         for frame in range(2):
             put_all(held_taps_one.at[frame], 0, flat(one_pad, frame, 0, 5), 0, brim)
             values = flat(one_pad, frame, rows, rows + 5)
             put_all(held_taps_one.at[frame], rows * pitch + EDGE, values, EDGE, 5 * pitch - EDGE)
         add_cached(0, held_taps_one, sum_one, pitch, [(0, brim), (rest, whole - rest)])
+
+    def held_edge_two():
         for frame in range(2):
             put_tile(held_taps_two.at[frame], 0, flat(two_pad, frame, 0, 3), 2)
             put_tile(held_taps_two.at[frame], rows, flat(two_pad, frame, rows, rows + 3), 2)
@@ -307,14 +316,28 @@
     def act(f, low, high):
         return norm_act(flat(x_pad, f, low, high), gains[0:1])
 
-    def conv_one(f, groups, again=False):
-        parts = [
+    def act_split(f, at):
+        put_all(taps_one, 0, act(f, 0, at + 1), 0, at * pitch)
+        put_all(taps_one, at * pitch, act(f, at - 1, rows + 5), pitch, (rows + 5 - at) * pitch)
+
+    def spans_one(groups):
+        return [
             (low * pitch, whole - low * pitch if low + height == rows + 2 else height * pitch + EDGE)
             for low, height in groups
         ]
-        fresh = product(taps_one, pitch, parts, matrix(0, f))
+
+    def spans_two(groups):
+        return [(low * cols, size * cols) for low, size in groups]
+
+    def multiply_one(f, groups):
+        return product(taps_one, pitch, spans_one(groups), matrix(0, f))
+
+    def multiply_two(f, groups):
+        return product(taps_two, cols, spans_two(groups), matrix(1, f))
+
+    def finish_one(f, groups, fresh, again=False):
         at = 0
-        for (low, height), (base, size) in zip(groups, parts):
+        for (low, height), (base, size) in zip(groups, spans_one(groups)):
             part = pl.ds(base, size)
             hidden = sum_one[f, part] + fresh[at : at + size, :channels]
             if f == 0:
@@ -323,19 +346,24 @@
             put_tile(taps_two, low, norm_act(hidden, gains[1:2]) * inside[part], height)
             at += size
 
-    def conv_two(f, groups):
-        parts = [(low * cols, size * cols) for low, size in groups]
-        fresh = product(taps_two, cols, parts, matrix(1, f))
+    def finish_two(f, groups, fresh):
         at = 0
-        for low, size in groups:
-            here = slice(at, at + size * cols)
-            part = pl.ds(low * cols, size * cols)
+        for (low, size), (base, count) in zip(groups, spans_two(groups)):
+            here, part = slice(at, at + count), pl.ds(base, count)
             branch = sum_two[f, part] + fresh[here, :channels]
             if f == 0:
                 sum_two[1, part] += fresh[here, channels:]
             inputs = x_pad[f, 2 + low : 2 + low + size, EDGE:].astype(jnp.float32)
             out[f, low : low + size] = (inputs + branch.reshape(size, cols, channels)).astype(out.dtype)
-            at += size * cols
+            at += count
+
+    def stage(f, ones, twos):
+        firsts = [multiply_one(f, groups) for groups in ones]
+        for groups, fresh in zip(ones, firsts):
+            finish_one(f, groups, fresh)
+        seconds = [multiply_two(f, groups) for groups in twos]
+        for groups, fresh in zip(twos, seconds):
+            finish_two(f, groups, fresh)
 
     def send_tile(f, groups):
         @pl.when(more)
@@ -350,38 +378,58 @@
     def _():
         received(begin[0], MID)
         put_all(taps_one, 3 * pitch, act(0, 3, rows + 2), 0, (rows - 1) * pitch)
-        conv_one(0, [(3, rows - 4)])
-        conv_two(0, middle)
+        stage(0, [[(3, rows - 4)]], [middle])
         if segments > 1:
             pl.semaphore_wait(ready_sem, plane)
         send_tile(0, middle)
         for stream in held + begin[:1]:
             received(stream, OUTER)
-        held_edges()
         put_all(taps_one, 0, act(0, 0, 5), 0, brim)
         put_all(taps_one, rows * pitch + EDGE, act(0, rows, rows + 5), EDGE, 5 * pitch - EDGE)
-        conv_one(0, [(0, 3), (rows - 1, 3)], again=True)
-        conv_two(0, borders)
+        held_edge_one()
+        ends = [(0, 3), (rows - 1, 3)]
+        fresh = multiply_one(0, ends)
+        held_edge_two()
+        finish_one(0, ends, fresh, again=True)
+        finish_two(0, borders, multiply_two(0, borders))
+        start(onward[0], more, (-1, 1))
+        send_tile(0, borders)
 
     @pl.when(later)
     def _():
-        for stream in held:
-            received(stream, OUTER)
-        held_edges()
+        received(held[0], OUTER)
+        held_edge_one()
+        received(held[1], OUTER)
+        held_edge_two()
         received(onward[0], OUTER)
         received(onward[0], MID, None, True)
-        put_all(taps_one, 0, act(0, 0, rows + 5), 0, (rows + 5) * pitch)
-        conv_one(0, [(0, edge + 2), (rows - edge, edge + 2)])
-        conv_two(0, borders)
-
-    start(onward[0], more, (-1, 1))
-    send_tile(0, borders)
-
-    @pl.when(later)
-    def _():
-        conv_one(0, [(edge + 2, rows - 2 * edge - 2)])
-        conv_two(0, middle)
+
+    @pl.when(later & more)
+    def _():
+        act_split(0, rows // 2 + 2)
+        tops, lows, mids = [(0, edge + 2)], [(rows - edge, edge + 2)], [(edge + 2, rows - 2 * edge - 2)]
+        top, low, mid = (multiply_one(0, groups) for groups in (tops, lows, mids))
+        finish_one(0, tops, top)
+        top = multiply_two(0, borders[:1])
+        finish_one(0, lows, low)
+        finish_one(0, mids, mid)
+        finish_two(0, borders[:1], top)
+        start(onward[0], True, (-1,))
+        send_tile(0, borders[:1])
+        low, mid = multiply_two(0, borders[1:]), multiply_two(0, middle)
+        finish_two(0, borders[1:], low)
+        start(onward[0], True, (1,))
+        send_tile(0, borders[1:])
+        finish_two(0, middle, mid)
         send_tile(0, middle)
+
+    half = rows // 2
+    halves = [[(0, half)], [(half, rows + 2 - half)]], [[(0, half - 2)], [(half - 2, rows + 2 - half)]]
+
+    @pl.when(later & ~more)
+    def _():
+        act_split(0, half + 3)
+        stage(0, *halves)
 
     start(onward[0], more, (0,))
 
@@ -389,10 +437,9 @@
         for group in (MID, OUTER):
             received(begin[f], group, first)
             received(onward[f], group, later, group == MID)
-        put_all(taps_one, 0, act(f, 0, rows + 5), 0, (rows + 5) * pitch)
-        conv_one(f, [(0, rows + 2)])
-        conv_two(f, [(0, rows)])
-        sent(onward[f - 1], more, True)
+        act_split(f, half + 3)
+        stage(f, *halves)
+        sent(onward[f - 1], more, True, (OUTER,))
         start(onward[f], more, (-1, 1))
         send_tile(f, borders + middle)
         start(onward[f], more, (0,))
@@ -401,7 +448,7 @@
         sent(stream)
     for f in range(total):
         sent(begin[f], first)
-    sent(onward[total - 1], more, True)
+        sent(onward[f], more, True, (MID,) if f + 1 < total else (MID, OUTER))
 
 
 def solution(mesh):

time: 23.5 us -> 22.5 us (0.957)
  Pallas kernels: 22.7 us -> 21.7 us
    pallas_call x1, Pallas kernels: 22.7 us -> 21.7 us  [on_device(): pl.pallas_call(functools.partial(kernel, counts), out_shape=pltpu.VMEM(fr...]
where the time goes in v3:
time: 22.5 us; the launch traced here: 22.4 us
  Pallas kernels  21.7 us (96%)
  local copies, waits for them, and re-layouts  0.66 us (3%)
    pallas_call x1, Pallas kernels, on_device(): pl.pallas_call(functools.partial(kernel, counts), out_shape=pltpu.VMEM(fr...  21.7 us
    unnamed x1, local copies, waits for them, and re-layouts  0.66 us

profile of v3, /device:TPU:29, one launch (start us, length us, event | category | flops | bytes accessed | tf_op | source)
XLA Modules:
  0.0 22.4 jit_solution(2552019208811311745)
XLA Ops:
  0.0 21.7 %shard_map.55 = bf16[2,16,16,128]{3,2,1,0:T(8,128)(2,1)S(1)} custom-call(bf16[2,16,16,128]{3,2,1,0:T(8,128)(2,1)} %frames.1, bf16[2,2,16,16,128]{4,3,2,1,0:T(8,128)(2,1)} %bitcast.7, bf16[2,3,1152,128]{3,2,1,0:T(8,128)(2,1)} %bitcast.6, f32[2,128]{1,0:T(2,128)} %bitcast.8, f32[2,128]{1,0:T(2,128)} %bitcast.9), custom_call_target="tpu_custom_call" | custom-call | tf_op jit(solution)/shard_map/pallas_call | solution.py:464
  21.7 0.7 %copy.7 = bf16[1,2,16,16,128]{4,3,2,1,0:T(8,128)(2,1)} copy(bf16[1,2,16,16,128]{4,3,2,1,0:T(8,128)(2,1)S(1)} %bitcast.5) | data formatting | bytes 262144

commit v4 on v3

--- a/solution.py
+++ b/solution.py
@@ -95,9 +95,9 @@
             device_id_type=pl.DeviceIdType.MESH,
         )
 
-    held = [(one_pad, one_pad, 2, 0, 0, 0), (two_pad, two_pad, 1, 1, 1, 0)]
-    begin = [(x_pad.at[f], x_pad.at[f], 2, 2 + f, 2 + f, 0) for f in range(total)]
-    onward = [(out.at[f], x_pad.at[f], 2, 2 + total + f, 2 + f, 1) for f in range(total)]
+    held = [(one_pad, one_pad, 2, 0, 0, 0), (two_pad, two_pad, 1, 0, 1, 0)]
+    begin = [(x_pad.at[f], x_pad.at[f], 2, 0, 2 + f, 0) for f in range(total)]
+    onward = [(out.at[f], x_pad.at[f], 2, 1 + f, 2 + f, 1) for f in range(total)]
 
     def start(stream, allowed, outer):
         for dr, dc in AROUND:
@@ -155,7 +155,7 @@
         return pltpu.make_async_remote_copy(
             src_ref=out.at[f, pl.ds(low, size)],
             dst_ref=x_pad.at[f, pl.ds(2 + low, size), pl.ds(EDGE, cols)],
-            send_sem=send_sem.at[2 + total + f, MID],
+            send_sem=send_sem.at[1 + f, MID],
             recv_sem=recv_sem.at[2 + f, MID],
             device_id=device(1, 0, 0),
             device_id_type=pl.DeviceIdType.MESH,
@@ -163,13 +163,9 @@
 
     centre_of = lambda pad, halo: pad.at[:, pl.ds(halo, rows), pl.ds(EDGE, cols)]
     own = local(frames, centre_of(x_pad, 2), 0)
-    held_copies = [local(caches.at[0], centre_of(one_pad, 2), 1), local(caches.at[1], centre_of(two_pad, 1), 2)]
-    parameters = [
-        local(biases_in, biases, 3),
-        local(gains_in, gains, 4),
-        local(weights_in.at[0], weights.at[0], 5),
-        local(weights_in.at[1], weights.at[1], 6),
-    ]
+    held_copies = [local(caches.at[0], centre_of(one_pad, 2), 1), local(caches.at[1], centre_of(two_pad, 1), 1)]
+    parameters = [local(biases_in, biases, 2), local(gains_in, gains, 2), local(weights_in, weights, 3)]
+    few = sum_one.at[0, pl.ds(0, biases.shape[0] + gains.shape[0])]
 
     @pl.when(first)
     def _():
@@ -206,18 +202,17 @@
     def _():
         own.wait()
 
-    for copy in held_copies:
-        copy.wait()
-    early = [(begin[0], first), (held[0], True), (held[1], True)]
+    local(caches, caches, 1).wait()
     even = row % 2 == 0
-    for stream, allowed in early:
-        start(stream, even & allowed, (-1,))
-        start(stream, ~even & allowed, (1,))
-    for stream, allowed in early:
-        start(stream, allowed, (0,))
-    for stream, allowed in early:
-        start(stream, even & allowed, (1,))
-        start(stream, ~even & allowed, (-1,))
+    for early in ([(held[0], True), (begin[0], first)], [(held[1], True)]):
+        for stream, allowed in early:
+            start(stream, even & allowed, (-1,))
+            start(stream, ~even & allowed, (1,))
+        for stream, allowed in early:
+            start(stream, allowed, (0,))
+        for stream, allowed in early:
+            start(stream, even & allowed, (1,))
+            start(stream, ~even & allowed, (-1,))
     for f in range(1, total):
         start(begin[f], first, (-1, 1, 0))
     signal_all(ready_sem, (-1,))
@@ -275,8 +270,8 @@
             sums[1, pl.ds(low, size)] = newer[here, channels:] + bias
             at += size
 
-    for copy in parameters:
-        copy.wait()
+    local(few, few, 2).wait()
+    parameters[-1].wait()
 
     whole = sum_one.shape[1]
     brim = -(-(3 * pitch + EDGE) // 16) * 16
@@ -382,17 +377,21 @@
         if segments > 1:
             pl.semaphore_wait(ready_sem, plane)
         send_tile(0, middle)
-        for stream in held + begin[:1]:
+        for stream in held[:1] + begin[:1]:
             received(stream, OUTER)
         put_all(taps_one, 0, act(0, 0, 5), 0, brim)
         put_all(taps_one, rows * pitch + EDGE, act(0, rows, rows + 5), EDGE, 5 * pitch - EDGE)
         held_edge_one()
         ends = [(0, 3), (rows - 1, 3)]
         fresh = multiply_one(0, ends)
+        received(held[1], OUTER)
         held_edge_two()
         finish_one(0, ends, fresh, again=True)
         finish_two(0, borders, multiply_two(0, borders))
-        start(onward[0], more, (-1, 1))
+        start(onward[0], even & more, (-1,))
+        start(onward[0], ~even & more, (1,))
+        start(onward[0], even & more, (1,))
+        start(onward[0], ~even & more, (-1,))
         send_tile(0, borders)
 
     @pl.when(later)
@@ -424,7 +423,10 @@
         send_tile(0, middle)
 
     half = rows // 2
-    halves = [[(0, half)], [(half, rows + 2 - half)]], [[(0, half - 2)], [(half - 2, rows + 2 - half)]]
+    third = (rows + 2) // 6 * 2
+    ones = [[(0, third)], [(third, third)], [(2 * third, rows + 2 - 2 * third)]]
+    twos = [[(0, third - 2)], [(third - 2, third)], [(2 * third - 2, rows + 2 - 2 * third)]]
+    halves = ones, twos
 
     @pl.when(later & ~more)
     def _():
@@ -439,16 +441,24 @@
             received(onward[f], group, later, group == MID)
         act_split(f, half + 3)
         stage(f, *halves)
-        sent(onward[f - 1], more, True, (OUTER,))
+        sent(onward[f - 1], later & more, True, (OUTER,))
         start(onward[f], more, (-1, 1))
         send_tile(f, borders + middle)
         start(onward[f], more, (0,))
 
-    for stream in held:
-        sent(stream)
+    for allowed, share in ((first, 4 + total), (later, 4)):
+        settle(
+            send_sem.at[0, MID], lambda up, side: cut(one_pad, rows, STRIP * side * share // 2),
+            (up_options, side_options), allowed,
+        )
+        height = 3 if share == 4 else 3 + total
+        settle(
+            send_sem.at[0, OUTER], lambda up, side: cut(one_pad, height * up, cols + STRIP * side),
+            (up_options, side_options), allowed,
+        )
     for f in range(total):
-        sent(begin[f], first)
-        sent(onward[f], more, True, (MID,) if f + 1 < total else (MID, OUTER))
+        sent(onward[f], first & more, True)
+        sent(onward[f], later & more, True, (MID,) if f + 1 < total else (MID, OUTER))
 
 
 def solution(mesh):
@@ -480,9 +490,9 @@
                 pltpu.VMEM((total, whole, channels), f32),
                 pltpu.VMEM((total, rows * cols, channels), f32),
                 pltpu.VMEM((whole, channels), f32),
-                pltpu.SemaphoreType.DMA((2 + 2 * total, 2)),
+                pltpu.SemaphoreType.DMA((1 + total, 2)),
                 pltpu.SemaphoreType.DMA((2 + total, 2)),
-                pltpu.SemaphoreType.DMA((7,)),
+                pltpu.SemaphoreType.DMA((4,)),
                 pltpu.SemaphoreType.REGULAR,
             ],
             compiler_params=pltpu.CompilerParams(collective_id=0, has_side_effects=True),

time: 22.5 us -> 22.4 us (level)
  no operation moved by 1% of the time
where the time goes in v4:
time: 22.4 us; the launch traced here: 22.2 us
  Pallas kernels  21.6 us (96%)
  local copies, waits for them, and re-layouts  0.66 us (3%)
    pallas_call x1, Pallas kernels, on_device(): pl.pallas_call(functools.partial(kernel, counts), out_shape=pltpu.VMEM(fr...  21.6 us
    unnamed x1, local copies, waits for them, and re-layouts  0.66 us

profile of v4, /device:TPU:29, one launch (start us, length us, event | category | flops | bytes accessed | tf_op | source)
XLA Modules:
  0.0 22.2 jit_solution(11035988334653425445)
XLA Ops:
  0.0 21.6 %shard_map.55 = bf16[2,16,16,128]{3,2,1,0:T(8,128)(2,1)S(1)} custom-call(bf16[2,16,16,128]{3,2,1,0:T(8,128)(2,1)} %frames.1, bf16[2,2,16,16,128]{4,3,2,1,0:T(8,128)(2,1)} %bitcast.7, bf16[2,3,1152,128]{3,2,1,0:T(8,128)(2,1)} %bitcast.6, f32[2,128]{1,0:T(2,128)} %bitcast.8, f32[2,128]{1,0:T(2,128)} %bitcast.9), custom_call_target="tpu_custom_call" | custom-call | tf_op jit(solution)/shard_map/pallas_call | solution.py:474
  21.6 0.7 %copy.7 = bf16[1,2,16,16,128]{4,3,2,1,0:T(8,128)(2,1)} copy(bf16[1,2,16,16,128]{4,3,2,1,0:T(8,128)(2,1)S(1)} %bitcast.5) | data formatting | bytes 262144

commit v5 on v4

--- a/solution.py
+++ b/solution.py
@@ -415,11 +415,10 @@
         finish_two(0, borders[:1], top)
         start(onward[0], True, (-1,))
         send_tile(0, borders[:1])
-        low, mid = multiply_two(0, borders[1:]), multiply_two(0, middle)
-        finish_two(0, borders[1:], low)
+        finish_two(0, borders[1:], multiply_two(0, borders[1:]))
         start(onward[0], True, (1,))
         send_tile(0, borders[1:])
-        finish_two(0, middle, mid)
+        finish_two(0, middle, multiply_two(0, middle))
         send_tile(0, middle)
 
     half = rows // 2

time: 22.4 us -> 22.2 us (level)
  no operation moved by 1% of the time
where the time goes in v5:
time: 22.2 us; the launch traced here: 22.1 us
  Pallas kernels  21.4 us (96%)
  local copies, waits for them, and re-layouts  0.66 us (3%)
    pallas_call x1, Pallas kernels, on_device(): pl.pallas_call(functools.partial(kernel, counts), out_shape=pltpu.VMEM(fr...  21.4 us
    unnamed x1, local copies, waits for them, and re-layouts  0.66 us

profile of v5, /device:TPU:29, one launch (start us, length us, event | category | flops | bytes accessed | tf_op | source)
XLA Modules:
  0.0 22.1 jit_solution(15166629969528902436)
XLA Ops:
  0.0 21.4 %shard_map.55 = bf16[2,16,16,128]{3,2,1,0:T(8,128)(2,1)S(1)} custom-call(bf16[2,16,16,128]{3,2,1,0:T(8,128)(2,1)} %frames.1, bf16[2,2,16,16,128]{4,3,2,1,0:T(8,128)(2,1)} %bitcast.7, bf16[2,3,1152,128]{3,2,1,0:T(8,128)(2,1)} %bitcast.6, f32[2,128]{1,0:T(2,128)} %bitcast.8, f32[2,128]{1,0:T(2,128)} %bitcast.9), custom_call_target="tpu_custom_call" | custom-call | tf_op jit(solution)/shard_map/pallas_call | solution.py:473
  21.4 0.7 %copy.7 = bf16[1,2,16,16,128]{4,3,2,1,0:T(8,128)(2,1)} copy(bf16[1,2,16,16,128]{4,3,2,1,0:T(8,128)(2,1)S(1)} %bitcast.5) | data formatting | bytes 262144
